TPU v7x, 32 devices: a whole 2x2x4 slice. The times are simulated.
32 devices in a mesh: ga: 2 (over x), row: 8 (over z, y), col: 2 (over core).
Axes of the slice: x: 2, y: 2, z: 4, core: 2. Of those that a mesh axis runs over, the one named last changes fastest.
Arguments:
- pair: bfloat16 [256, 128, 128], P(('ga', 'row', 'col')), parts along dimension 0, may hold values from -480 to 480
- residue_mask: int32 [256], P('ga'), parts along dimension 0, may hold values from 0 to 1, as said below
- targets: int32 [256, 128], P(('ga', 'row', 'col')), parts along dimension 0, may hold values from 0 to 63
- ln_gain: float32 [2, 128], replicated, may hold values from 0.25 to 1.75
- ln_shift: float32 [2, 128], replicated, may hold values from -3 to 3
- w_in: bfloat16 [5, 128, 128], P(None, None, 'col'), may hold values from -0.5 to 0.5
- b_in: float32 [5, 128], replicated, may hold values from -3 to 3
- w_out: bfloat16 [128, 128], P('col'), may hold values from -0.5 to 0.5
- b_out: float32 [128], replicated, may hold values from -3 to 3
- head_weight: bfloat16 [128, 64], replicated, may hold values from -0.5 to 0.5
- head_bias: float32 [64], replicated, may hold values from -4 to 4
Outputs:
- update: bfloat16 [256, 128, 128], P(('ga', 'row', 'col')), parts along dimension 0
- pair_loss: float32 [256, 128], P(('ga', 'row', 'col')), parts along dimension 0
There are 2 independent parts, one for each index of `ga`. A program takes and returns all parts, laid end to end along the dimension named above; an argument that names none is the same for every part. Nothing has to cross between parts.
Inputs may be any that keep to these rules, and one draw needn't show every extreme that they name: `residue_mask`: each part's entries are 1 for residues 0 to some length - 1 and 0 after it; the length is at least 64 and at most 128.
All inputs are finite; a program needn't handle non-finite values.
Results may differ from a plain program's by a relative error of at most 0.0055.
Values may be sent and summed in bfloat16 or wider, within the bound.
A program may use at most 64 MiB of HBM per device.

v0:
```python
import jax
import jax.numpy as jnp
from jax import lax
from jax.sharding import PartitionSpec as P


def normalize(values, gain_vec, shift_vec, epsilon, reduce_axis):
    average = jnp.mean(values, axis=reduce_axis, keepdims=True)
    centred = values - average
    spread = jnp.mean(centred * centred, axis=reduce_axis, keepdims=True)
    return centred * lax.rsqrt(spread + epsilon) * gain_vec + shift_vec


def local(
    pair, residue_mask, targets, ln_gain, ln_shift, w_in, b_in, w_out, b_out, head_weight, head_bias
):
    row_count, length, pair_width = pair.shape
    groups = lax.axis_size(("row", "col"))
    chan_share = pair_width // groups
    res_mask = residue_mask.astype(jnp.float32)
    own_mask = lax.dynamic_slice_in_dim(
        res_mask, lax.axis_index(("row", "col")) * row_count, row_count
    )
    pair_mask = own_mask[:, None] * res_mask[None, :]
    normed = normalize(pair.astype(jnp.float32), ln_gain[0], ln_shift[0], 0.1, -1).astype(
        jnp.bfloat16
    )
    projected = jnp.einsum(
        "ikc,ncd->ndik",
        normed,
        lax.all_gather(w_in, "col", axis=2, tiled=True),
        preferred_element_type=jnp.float32,
    )
    projected = projected + b_in[:, :, None, None]
    left_side = pair_mask * jax.nn.sigmoid(projected[1]) * projected[0]
    right_side = pair_mask * jax.nn.sigmoid(projected[3]) * projected[2]
    stacked = jnp.stack([left_side, right_side, projected[4]])
    left_side = stacked[0].astype(jnp.bfloat16)
    right_side = stacked[1].astype(jnp.bfloat16)
    gate_pre = stacked[2]
    left_blocks = left_side.reshape(groups, chan_share, row_count, length)
    right_blocks = right_side.reshape(groups, chan_share, row_count, length)
    left_part = lax.all_to_all(left_blocks, ("row", "col"), split_axis=0, concat_axis=2, tiled=True)
    right_part = lax.all_to_all(
        right_blocks, ("row", "col"), split_axis=0, concat_axis=2, tiled=True
    )
    product = jnp.einsum(
        "xcik,xcjk->xcij", left_part, right_part, preferred_element_type=jnp.float32
    )
    returned = lax.all_to_all(
        product.astype(jnp.bfloat16), ("row", "col"), split_axis=2, concat_axis=0, tiled=True
    )
    outer_prod = returned.reshape(pair_width, row_count, length)
    normed_outer = normalize(
        outer_prod.astype(jnp.float32),
        ln_gain[1][:, None, None],
        ln_shift[1][:, None, None],
        1.0,
        0,
    ).astype(jnp.bfloat16)
    mixed = jnp.einsum(
        "cij,cd->dij",
        normed_outer,
        lax.all_gather(w_out, "col", axis=0, tiled=True),
        preferred_element_type=jnp.float32,
    )
    update_chan = jax.nn.sigmoid(gate_pre) * (mixed + b_out[:, None, None])
    update = jnp.transpose(update_chan, (1, 2, 0)).astype(jnp.bfloat16)
    new_pair = (pair.astype(jnp.float32) + update.astype(jnp.float32)).astype(jnp.bfloat16)
    logits = (
        jnp.einsum("ijc,cb->ijb", new_pair, head_weight, preferred_element_type=jnp.float32)
        + head_bias
    )
    mirrored = lax.all_to_all(
        logits.astype(jnp.bfloat16), ("row", "col"), split_axis=1, concat_axis=0, tiled=True
    ).astype(logits.dtype)
    symmetric = logits + jnp.transpose(mirrored, (1, 0, 2))
    row_top = jnp.max(symmetric, axis=-1, keepdims=True)
    log_total = row_top[..., 0] + jnp.log(jnp.sum(jnp.exp(symmetric - row_top), axis=-1))
    bin_index = jnp.arange(symmetric.shape[2], dtype=jnp.int32)
    picked = jnp.sum(jnp.where(targets[..., None] == bin_index, symmetric, 0.0), axis=-1)
    pair_loss = pair_mask * (log_total - picked)
    return (update, pair_loss)


def solution(mesh):
    placed = (
        P(("ga", "row", "col"), None, None),
        P("ga"),
        P(("ga", "row", "col"), None),
        P(),
        P(),
        P(None, None, "col"),
        P(),
        P("col", None),
        P(),
        P(),
        P(),
    )
    return jax.shard_map(
        local,
        mesh=mesh,
        in_specs=placed,
        out_specs=(P(("ga", "row", "col"), None, None), P(("ga", "row", "col"), None)),
        check_vma=False,
    )
```

profile of v0, /device:TPU:0, one launch (start us, length us, event | category | flops | bytes accessed | tf_op | source)
XLA Modules:
  0.0 68.8 jit_solution(7911302540243961104)
XLA Ops:
  0.6 1.1 %copy.51 = bf16[8,128,128]{1,2,0:T(8,128)(2,1)S(1)} copy(bf16[8,128,128]{2,1,0:T(8,128)(2,1)} %param.11) | data formatting | bytes 524288 | tf_op args[0]
  1.9 2.3 %all_gather.6 = bf16[5,128,128]{1,2,0:T(8,128)(2,1)S(1)} all-gather(bf16[5,128,64]{1,2,0:T(8,128)(2,1)} %param.16), channel_id=1, replica_groups=mesh['ga'=2,'row'=8,'col'=2] {'col'}, dimensions={2}, use_global_device_ids=true | all-gather | bytes 245760 | tf_op jit(solution)/shard_map/all_gather | solution.py:31
  4.2 0.8 %slice_bitcast_fusion.2 = (f32[128]{0:T(128)S(1)}, f32[128]{0:T(128)S(1)}, f32[128]{0:T(128)S(1)}, f32[128]{0:T(128)S(1)}) fusion(f32[2,128]{1,0:T(2,128)} %param.15, f32[2,128]{1,0:T(2,128)} %param.14), kind=kLoop, calls=%fused_computation.74 | loop fusion | bytes 4096 | tf_op jit(solution)/shard_map/add | solution.py:11
  5.0 1.3 %add_bitcast_fusion = f32[5,128,8,128]{3,1,0,2:T(8,128)S(1)} fusion(f32[5,128]{1,0:T(8,128)} %param.17, bf16[8,128,128]{1,2,0:T(8,128)(2,1)S(1)} %copy.51, f32[128]{0:T(128)S(1)} %get-tuple-element.21, f32[128]{0:T(128)S(1)} %get-tuple-element.24, f32[8,128]{1,0:T(8,128)S(1)} %add_rsqrt_fusion.1, f32[8,128]{1,0:T(8,128)S(1)} %broadcast_multiply_fusion.2, ...), kind=kOutput, calls=%fused_computation | convolution fusion | flops 169213952 | bytes 3059200 | tf_op jit(solution)/shard_map/ikc,ncd->ndik/dot_general | solution.py:28
  6.3 1.3 %fusion.19 = (f32[16,8,8,128]{3,1,0,2:T(8,128)S(1)}, f32[16,8,8,128]{3,1,0,2:T(8,128)}, f32[16,8,8,128]{3,1,0,2:T(8,128)}, f32[16,8,8,128]{3,1,0,2:T(8,128)}) fusion(f32[5,128,8,128]{3,1,0,2:T(8,128)S(1)} %add_bitcast_fusion), kind=kLoop, calls=%fused_computation.30 | loop fusion | flops 786432 | bytes 4194304 | tf_op jit(solution)/shard_map/div | solution.py:35
  7.7 1.5 %fusion.29 = (bf16[16,8,8,128]{3,1,2,0:T(8,128)(2,1)S(1)}, bf16[16,8,8,128]{3,1,2,0:T(8,128)(2,1)S(1)}) fusion(f32[16,8,8,128]{3,1,0,2:T(8,128)} %get-tuple-element.15, f32[16,8,8,128]{3,1,0,2:T(8,128)S(1)} %get-tuple-element.12, f32[8,128]{1,0:T(8,128)S(1)} %broadcast_multiply_fusion, f32[16,8,8,128]{3,1,0,2:T(8,128)} %get-tuple-element.13, ...), kind=kLoop, calls=%fused_computation.47 | loop fusion | flops 786432 | bytes 2625536 | tf_op jit(solution)/shard_map/convert_element_type | solution.py:38
  9.2 17.1 %all_to_all.48 = bf16[16,8,8,128]{3,1,2,0:T(8,128)(2,1)S(1)} all-to-all(bf16[16,8,8,128]{3,1,2,0:T(8,128)(2,1)S(1)} %get-tuple-element.17), channel_id=1, replica_groups=mesh['ga'=2,'row'=8,'col'=2] {'row','col'}, dimensions={0} | all-to-all | bytes 524288 | tf_op jit(solution)/shard_map/all_to_all | solution.py:44
  26.3 12.7 %all_to_all.49 = bf16[16,8,8,128]{3,1,2,0:T(8,128)(2,1)S(1)} all-to-all(bf16[16,8,8,128]{3,1,2,0:T(8,128)(2,1)S(1)} %get-tuple-element.16), channel_id=1, replica_groups=mesh['ga'=2,'row'=8,'col'=2] {'row','col'}, dimensions={0} | all-to-all | bytes 524288 | tf_op jit(solution)/shard_map/all_to_all | solution.py:43
  39.0 0.3 fusion.3
  39.3 0.9 %copy.59 = bf16[1,8,128,128]{3,1,0,2:T(8,128)(2,1)} copy(bf16[1,8,128,128]{3,2,1,0:T(8,128)(2,1)S(1)} %fusion.3) | data formatting | bytes 524288 | tf_op jit(solution)/shard_map/convert_element_type | solution.py:51
  40.2 3.5 %all-to-all-start.2 = ((bf16[1,8,128,128]{3,1,0,2:T(8,128)(2,1)}), bf16[1,8,128,128]{3,1,0,2:T(8,128)(2,1)S(1)}, u32[]{:S(2)}, u32[]{:S(2)}) async-start(bf16[1,8,128,128]{3,1,0,2:T(8,128)(2,1)} %copy.59), calls=%async_computation.2 | async-start | bytes 524288 | tf_op jit(solution)/shard_map/all_to_all | solution.py:50
  43.8 1.8 %all_gather.7 = bf16[128,128]{1,0:T(8,128)(2,1)S(1)} all-gather(bf16[64,128]{1,0:T(8,128)(2,1)S(1)} %copy-done.1), channel_id=1, replica_groups=mesh['ga'=2,'row'=8,'col'=2] {'col'}, dimensions={0}, use_global_device_ids=true | all-gather | bytes 49152 | tf_op jit(solution)/shard_map/all_gather | solution.py:64
  45.6 8.1 %all-to-all-done.2 = bf16[1,8,128,128]{3,1,0,2:T(8,128)(2,1)S(1)} async-done(((bf16[1,8,128,128]{3,1,0,2:T(8,128)(2,1)}), bf16[1,8,128,128]{3,1,0,2:T(8,128)(2,1)S(1)}, u32[]{:S(2)}, u32[]{:S(2)}) %all-to-all-start.2) | async-done | bytes 262176 | tf_op jit(solution)/shard_map/all_to_all | solution.py:50
  54.1 0.3 fusion.27
  54.5 0.3 fusion.4
  54.8 0.2 fusion.47
  55.0 0.2 copy.65
  55.2 0.9 %reshape.121 = bf16[16,2,2048]{2,1,0:T(2,128)(2,1)} reshape(bf16[128,8,64]{2,1,0:T(8,128)(2,1)S(1)} %bitcast.103) | data formatting | bytes 262144
  56.1 3.5 %all-to-all-start.3 = ((bf16[16,2,2048]{2,1,0:T(2,128)(2,1)}), bf16[16,2,2048]{2,1,0:T(2,128)(2,1)S(1)}, u32[]{:S(2)}, u32[]{:S(2)}) async-start(bf16[16,2,2048]{2,1,0:T(2,128)(2,1)} %reshape.121), calls=%async_computation.3 | async-start | bytes 262144 | tf_op jit(solution)/shard_map/all_to_all | solution.py:74
  59.6 0.9 %copy.69 = bf16[8,128,128]{2,1,0:T(8,128)(2,1)} copy(bf16[8,128,128]{1,2,0:T(8,128)(2,1)S(1)} %fusion.4) | data formatting | bytes 524288
  60.5 7.0 %all-to-all-done.3 = bf16[16,2,2048]{2,1,0:T(2,128)(2,1)S(1)} async-done(((bf16[16,2,2048]{2,1,0:T(2,128)(2,1)}), bf16[16,2,2048]{2,1,0:T(2,128)(2,1)S(1)}, u32[]{:S(2)}, u32[]{:S(2)}) %all-to-all-start.3) | async-done | bytes 131104 | tf_op jit(solution)/shard_map/all_to_all | solution.py:74
  67.5 0.2 reshape.122
  67.8 0.2 copy.68
  68.2 0.7 subtract_multiply_fusion
  (29 shorter events, 0.9 us)
Async XLA Ops:
  0.6 54.2 %copy-start = (bf16[128,64]{0,1:T(8,128)(2,1)S(1)}, bf16[128,64]{0,1:T(8,128)(2,1)}, u32[]{:S(2)}) copy-start(bf16[128,64]{0,1:T(8,128)(2,1)} %param.20) | copy-start | bytes 49156
  6.2 1.3 %copy-start.4 = (s32[128]{0:T(128)S(1)}, s32[128]{0:T(128)}, u32[]{:S(2)}) copy-start(s32[128]{0:T(128)} %param.12) | copy-start | bytes 1540
  7.7 36.0 %copy-start.1 = (bf16[64,128]{1,0:T(8,128)(2,1)S(1)}, bf16[64,128]{1,0:T(8,128)(2,1)}, u32[]{:S(2)}) copy-start(bf16[64,128]{1,0:T(8,128)(2,1)} %param.18) | copy-start | bytes 49156
  39.0 15.4 %copy-start.5 = (f32[128]{0:T(128)S(1)}, f32[128]{0:T(128)}, u32[]{:S(2)}) copy-start(f32[128]{0:T(128)} %param.19) | copy-start | bytes 1540
  40.2 13.5 %all-to-all-start.2 = ((bf16[1,8,128,128]{3,1,0,2:T(8,128)(2,1)}), bf16[1,8,128,128]{3,1,0,2:T(8,128)(2,1)S(1)}, u32[]{:S(2)}, u32[]{:S(2)}) async-start(bf16[1,8,128,128]{3,1,0,2:T(8,128)(2,1)} %copy.59), calls=%async_computation.2 | async-start | bytes 524288 | tf_op jit(solution)/shard_map/all_to_all | solution.py:50
  54.0 0.8 %copy-start.3 = (f32[64]{0:T(128)S(1)}, f32[64]{0:T(128)}, u32[]{:S(2)}) copy-start(f32[64]{0:T(128)} %param.21) | copy-start | bytes 772
  55.0 13.1 %copy-start.2 = (s32[8,128]{1,0:T(8,128)S(1)}, s32[8,128]{1,0:T(8,128)}, u32[]{:S(2)}) copy-start(s32[8,128]{1,0:T(8,128)} %param.13) | copy-start | bytes 12292
  56.1 11.4 %all-to-all-start.3 = ((bf16[16,2,2048]{2,1,0:T(2,128)(2,1)}), bf16[16,2,2048]{2,1,0:T(2,128)(2,1)S(1)}, u32[]{:S(2)}, u32[]{:S(2)}) async-start(bf16[16,2,2048]{2,1,0:T(2,128)(2,1)} %reshape.121), calls=%async_computation.3 | async-start | bytes 262144 | tf_op jit(solution)/shard_map/all_to_all | solution.py:74
where the time goes:
time: 69.3 us; the launch traced here: 68.8 us
  blocking collectives  33.9 us (49%)
  waiting for transfers between devices  15.2 us (22%)
  starting transfers between devices  7.04 us (10%)
  local copies, waits for them, and re-layouts  5.29 us (8%)
  other arithmetic  4.54 us (7%)
  matrix products  2.07 us (3%)
  between operations  0.87 us (1%)
    all_to_all x1, blocking collectives, local(): lax.all_to_all(right_blocks, ('row', 'col'), split_axis=0, concat_axis=2,...  17.1 us
    all_to_all x1, blocking collectives, local(): lax.all_to_all(left_blocks, ('row', 'col'), split_axis=0, concat_axis=2,...  12.7 us
    all_to_all x1, waiting for transfers between devices, local(): lax.all_to_all(product.astype(jnp.bfloat16), ('row', 'col'), split_axis=2...  8.14 us
    all_to_all x1, waiting for transfers between devices, local(): lax.all_to_all(logits.astype(jnp.bfloat16), ('row', 'col'), split_axis=1,...  7.02 us
    all_to_all x1, starting transfers between devices, local(): lax.all_to_all(product.astype(jnp.bfloat16), ('row', 'col'), split_axis=2...  3.53 us
    all_to_all x1, starting transfers between devices, local(): lax.all_to_all(logits.astype(jnp.bfloat16), ('row', 'col'), split_axis=1,...  3.51 us
    unnamed x16, local copies, waits for them, and re-layouts  3.09 us
    all_gather x1, blocking collectives, local(): lax.all_gather(w_in, 'col', axis=2, tiled=True)  2.27 us
  transfers between devices with their start and end apart: 2, of which 2 were waited for; matrix products, arithmetic and copies ran while one was open for 1% of the time, Pallas kernels for 0%

commit v1 on v0

--- a/solution.py
+++ b/solution.py
@@ -2,6 +2,12 @@
 import jax.numpy as jnp
 from jax import lax
 from jax.sharding import PartitionSpec as P
+
+
+def stacked_exchange(x, axis, split, join):
+    pieces = jnp.split(x, lax.axis_size(axis), axis=split)
+    got = lax.all_to_all(jnp.stack(pieces), axis, 0, 0)
+    return jnp.concatenate(got, axis=join)
 
 
 def normalize(values, gain_vec, shift_vec, epsilon, reduce_axis):
@@ -71,9 +77,9 @@
         jnp.einsum("ijc,cb->ijb", new_pair, head_weight, preferred_element_type=jnp.float32)
         + head_bias
     )
-    mirrored = lax.all_to_all(
-        logits.astype(jnp.bfloat16), ("row", "col"), split_axis=1, concat_axis=0, tiled=True
-    ).astype(logits.dtype)
+    mirrored = stacked_exchange(logits.astype(jnp.bfloat16), ("row", "col"), 1, 0).astype(
+        logits.dtype
+    )
     symmetric = logits + jnp.transpose(mirrored, (1, 0, 2))
     row_top = jnp.max(symmetric, axis=-1, keepdims=True)
     log_total = row_top[..., 0] + jnp.log(jnp.sum(jnp.exp(symmetric - row_top), axis=-1))

time: 69.3 us -> 71.6 us (1.033)
  local copies, waits for them, and re-layouts: 5.29 us -> 7.45 us
    another operation x0 -> x18, local copies, waits for them, and re-layouts: none -> 2.27 us  [stacked_exchange(): got = lax.all_to_all(jnp.stack(pieces), axis, 0, 0)]
    unnamed x16 -> x31, local copies, waits for them, and re-layouts: 3.09 us -> 3.23 us
where the time goes in v1:
time: 71.6 us; the launch traced here: 71.1 us
  blocking collectives  33.9 us (47%)
  waiting for transfers between devices  15.2 us (21%)
  local copies, waits for them, and re-layouts  7.45 us (10%)
  starting transfers between devices  7.04 us (10%)
  other arithmetic  4.57 us (6%)
  matrix products  2.07 us (3%)
  between operations  0.94 us (1%)
    all_to_all x1, blocking collectives, local(): lax.all_to_all(right_blocks, ('row', 'col'), split_axis=0, concat_axis=2,...  17.1 us
    all_to_all x1, blocking collectives, local(): lax.all_to_all(left_blocks, ('row', 'col'), split_axis=0, concat_axis=2,...  12.7 us
    all_to_all x1, waiting for transfers between devices, local(): lax.all_to_all(product.astype(jnp.bfloat16), ('row', 'col'), split_axis=2...  8.14 us
    all_to_all x1, waiting for transfers between devices, stacked_exchange(): got = lax.all_to_all(jnp.stack(pieces), axis, 0, 0)  7.02 us
    all_to_all x1, starting transfers between devices, local(): lax.all_to_all(product.astype(jnp.bfloat16), ('row', 'col'), split_axis=2...  3.53 us
    all_to_all x1, starting transfers between devices, stacked_exchange(): got = lax.all_to_all(jnp.stack(pieces), axis, 0, 0)  3.51 us
    unnamed x31, local copies, waits for them, and re-layouts  3.23 us
    all_gather x1, blocking collectives, local(): lax.all_gather(w_in, 'col', axis=2, tiled=True)  2.27 us
  transfers between devices with their start and end apart: 2, of which 2 were waited for; matrix products, arithmetic and copies ran while one was open for 1% of the time, Pallas kernels for 0%

profile of v1, /device:TPU:0, one launch (start us, length us, event | category | flops | bytes accessed | tf_op | source)
XLA Modules:
  0.0 71.1 jit_solution(11830761542855965868)
XLA Ops:
  0.6 1.1 %copy.63 = bf16[8,128,128]{1,2,0:T(8,128)(2,1)S(1)} copy(bf16[8,128,128]{2,1,0:T(8,128)(2,1)} %param.11) | data formatting | bytes 524288 | tf_op args[0]
  1.9 2.3 %all_gather.6 = bf16[5,128,128]{1,2,0:T(8,128)(2,1)S(1)} all-gather(bf16[5,128,64]{1,2,0:T(8,128)(2,1)} %param.16), channel_id=1, replica_groups=mesh['ga'=2,'row'=8,'col'=2] {'col'}, dimensions={2}, use_global_device_ids=true | all-gather | bytes 245760 | tf_op jit(solution)/shard_map/all_gather | solution.py:37
  4.2 0.8 %slice_bitcast_fusion.18 = (f32[128]{0:T(128)S(1)}, f32[128]{0:T(128)S(1)}, f32[128]{0:T(128)S(1)}, f32[128]{0:T(128)S(1)}) fusion(f32[2,128]{1,0:T(2,128)} %param.15, f32[2,128]{1,0:T(2,128)} %param.14), kind=kLoop, calls=%fused_computation.106 | loop fusion | bytes 4096 | tf_op jit(solution)/shard_map/add | solution.py:17
  5.0 1.3 %add_bitcast_fusion = f32[5,128,8,128]{3,1,0,2:T(8,128)S(1)} fusion(f32[5,128]{1,0:T(8,128)} %param.17, bf16[8,128,128]{1,2,0:T(8,128)(2,1)S(1)} %copy.63, f32[128]{0:T(128)S(1)} %get-tuple-element.37, f32[128]{0:T(128)S(1)} %get-tuple-element.40, f32[8,128]{1,0:T(8,128)S(1)} %add_rsqrt_fusion.1, f32[8,128]{1,0:T(8,128)S(1)} %broadcast_multiply_fusion.2, ...), kind=kOutput, calls=%fused_computation | convolution fusion | flops 169213952 | bytes 3059200 | tf_op jit(solution)/shard_map/ikc,ncd->ndik/dot_general | solution.py:34
  6.3 1.3 %fusion.19 = (f32[16,8,8,128]{3,1,0,2:T(8,128)S(1)}, f32[16,8,8,128]{3,1,0,2:T(8,128)}, f32[16,8,8,128]{3,1,0,2:T(8,128)}, f32[16,8,8,128]{3,1,0,2:T(8,128)}) fusion(f32[5,128,8,128]{3,1,0,2:T(8,128)S(1)} %add_bitcast_fusion), kind=kLoop, calls=%fused_computation.30 | loop fusion | flops 786432 | bytes 4194304 | tf_op jit(solution)/shard_map/div | solution.py:41
  7.7 1.5 %fusion.29 = (bf16[16,8,8,128]{3,1,2,0:T(8,128)(2,1)S(1)}, bf16[16,8,8,128]{3,1,2,0:T(8,128)(2,1)S(1)}) fusion(f32[16,8,8,128]{3,1,0,2:T(8,128)} %get-tuple-element.15, f32[16,8,8,128]{3,1,0,2:T(8,128)S(1)} %get-tuple-element.12, f32[8,128]{1,0:T(8,128)S(1)} %broadcast_multiply_fusion, f32[16,8,8,128]{3,1,0,2:T(8,128)} %get-tuple-element.13, ...), kind=kLoop, calls=%fused_computation.46 | loop fusion | flops 786432 | bytes 2625536 | tf_op jit(solution)/shard_map/convert_element_type | solution.py:44
  9.3 17.1 %all_to_all.44 = bf16[16,8,8,128]{3,1,2,0:T(8,128)(2,1)S(1)} all-to-all(bf16[16,8,8,128]{3,1,2,0:T(8,128)(2,1)S(1)} %get-tuple-element.33), channel_id=1, replica_groups=mesh['ga'=2,'row'=8,'col'=2] {'row','col'}, dimensions={0} | all-to-all | bytes 524288 | tf_op jit(solution)/shard_map/all_to_all | solution.py:50
  26.4 12.7 %all_to_all.45 = bf16[16,8,8,128]{3,1,2,0:T(8,128)(2,1)S(1)} all-to-all(bf16[16,8,8,128]{3,1,2,0:T(8,128)(2,1)S(1)} %get-tuple-element.32), channel_id=1, replica_groups=mesh['ga'=2,'row'=8,'col'=2] {'row','col'}, dimensions={0} | all-to-all | bytes 524288 | tf_op jit(solution)/shard_map/all_to_all | solution.py:49
  39.0 0.3 fusion.3
  39.3 0.9 %copy.71 = bf16[1,8,128,128]{3,1,0,2:T(8,128)(2,1)} copy(bf16[1,8,128,128]{3,2,1,0:T(8,128)(2,1)S(1)} %fusion.3) | data formatting | bytes 524288 | tf_op jit(solution)/shard_map/convert_element_type | solution.py:57
  40.2 3.5 %all-to-all-start.2 = ((bf16[1,8,128,128]{3,1,0,2:T(8,128)(2,1)}), bf16[1,8,128,128]{3,1,0,2:T(8,128)(2,1)S(1)}, u32[]{:S(2)}, u32[]{:S(2)}) async-start(bf16[1,8,128,128]{3,1,0,2:T(8,128)(2,1)} %copy.71), calls=%async_computation.2 | async-start | bytes 524288 | tf_op jit(solution)/shard_map/all_to_all | solution.py:56
  43.8 1.8 %all_gather.7 = bf16[128,128]{1,0:T(8,128)(2,1)S(1)} all-gather(bf16[64,128]{1,0:T(8,128)(2,1)S(1)} %copy-done.1), channel_id=1, replica_groups=mesh['ga'=2,'row'=8,'col'=2] {'col'}, dimensions={0}, use_global_device_ids=true | all-gather | bytes 49152 | tf_op jit(solution)/shard_map/all_gather | solution.py:70
  45.6 8.1 %all-to-all-done.2 = bf16[1,8,128,128]{3,1,0,2:T(8,128)(2,1)S(1)} async-done(((bf16[1,8,128,128]{3,1,0,2:T(8,128)(2,1)}), bf16[1,8,128,128]{3,1,0,2:T(8,128)(2,1)S(1)}, u32[]{:S(2)}, u32[]{:S(2)}) %all-to-all-start.2) | async-done | bytes 262176 | tf_op jit(solution)/shard_map/all_to_all | solution.py:56
  54.1 0.3 fusion.27
  54.5 0.3 fusion.4
  54.8 0.2 fusion.47
  55.0 0.6 slice_bitcast_fusion.2
  57.5 0.9 %reshape.119 = bf16[16,2,2048]{2,1,0:T(2,128)(2,1)} reshape(bf16[16,8,8,64]{3,2,1,0:T(8,128)(2,1)S(1)} %constant_dynamic-update-slice_fusion) | data formatting | bytes 262144
  58.4 3.5 %all-to-all-start.3 = ((bf16[16,2,2048]{2,1,0:T(2,128)(2,1)}), bf16[16,2,2048]{2,1,0:T(2,128)(2,1)S(1)}, u32[]{:S(2)}, u32[]{:S(2)}) async-start(bf16[16,2,2048]{2,1,0:T(2,128)(2,1)} %reshape.119), calls=%async_computation.3 | async-start | bytes 262144 | tf_op jit(solution)/shard_map/all_to_all | solution.py:9
  61.9 0.8 %copy.94 = bf16[8,128,128]{2,1,0:T(8,128)(2,1)} copy(bf16[8,128,128]{1,2,0:T(8,128)(2,1)S(1)} %fusion.4) | data formatting | bytes 524288
  62.8 7.0 %all-to-all-done.3 = bf16[16,2,2048]{2,1,0:T(2,128)(2,1)S(1)} async-done(((bf16[16,2,2048]{2,1,0:T(2,128)(2,1)}), bf16[16,2,2048]{2,1,0:T(2,128)(2,1)S(1)}, u32[]{:S(2)}, u32[]{:S(2)}) %all-to-all-start.3) | async-done | bytes 131104 | tf_op jit(solution)/shard_map/all_to_all | solution.py:9
  69.8 0.2 reshape.120
  70.1 0.2 copy.93
  70.4 0.7 subtract_multiply_fusion
  (60 shorter events, 2.7 us)
Async XLA Ops:
  0.6 54.2 %copy-start = (bf16[128,64]{0,1:T(8,128)(2,1)S(1)}, bf16[128,64]{0,1:T(8,128)(2,1)}, u32[]{:S(2)}) copy-start(bf16[128,64]{0,1:T(8,128)(2,1)} %param.20) | copy-start | bytes 49156
  6.2 1.3 %copy-start.4 = (s32[128]{0:T(128)S(1)}, s32[128]{0:T(128)}, u32[]{:S(2)}) copy-start(s32[128]{0:T(128)} %param.12) | copy-start | bytes 1540
  7.7 36.0 %copy-start.1 = (bf16[64,128]{1,0:T(8,128)(2,1)S(1)}, bf16[64,128]{1,0:T(8,128)(2,1)}, u32[]{:S(2)}) copy-start(bf16[64,128]{1,0:T(8,128)(2,1)} %param.18) | copy-start | bytes 49156
  39.0 15.4 %copy-start.5 = (f32[128]{0:T(128)S(1)}, f32[128]{0:T(128)}, u32[]{:S(2)}) copy-start(f32[128]{0:T(128)} %param.19) | copy-start | bytes 1540
  40.2 13.5 %all-to-all-start.2 = ((bf16[1,8,128,128]{3,1,0,2:T(8,128)(2,1)}), bf16[1,8,128,128]{3,1,0,2:T(8,128)(2,1)S(1)}, u32[]{:S(2)}, u32[]{:S(2)}) async-start(bf16[1,8,128,128]{3,1,0,2:T(8,128)(2,1)} %copy.71), calls=%async_computation.2 | async-start | bytes 524288 | tf_op jit(solution)/shard_map/all_to_all | solution.py:56
  54.0 0.8 %copy-start.3 = (f32[64]{0:T(128)S(1)}, f32[64]{0:T(128)}, u32[]{:S(2)}) copy-start(f32[64]{0:T(128)} %param.21) | copy-start | bytes 772
  56.6 13.8 %copy-start.2 = (s32[8,128]{1,0:T(8,128)S(1)}, s32[8,128]{1,0:T(8,128)}, u32[]{:S(2)}) copy-start(s32[8,128]{1,0:T(8,128)} %param.13) | copy-start | bytes 12292
  58.4 11.4 %all-to-all-start.3 = ((bf16[16,2,2048]{2,1,0:T(2,128)(2,1)}), bf16[16,2,2048]{2,1,0:T(2,128)(2,1)S(1)}, u32[]{:S(2)}, u32[]{:S(2)}) async-start(bf16[16,2,2048]{2,1,0:T(2,128)(2,1)} %reshape.119), calls=%async_computation.3 | async-start | bytes 262144 | tf_op jit(solution)/shard_map/all_to_all | solution.py:9
